TPU v7x, 512 devices: a whole 4x8x8 slice. The times are simulated.
512 devices in a mesh: row: 16 (over y_lo, x), col: 8 (over z), vol: 4 (over y_hi, core).
Axes of the slice: x: 4, y: 8 (y_hi: 2, y_lo: 4; y = y_hi * 4 + y_lo), z: 8, core: 2. Of those that a mesh axis runs over, the one named last changes fastest.
Arguments:
- panel: bfloat16 [2048, 131072], P('row', ('col', 'vol')), may hold values from -0.015625 to 0.015625
- density: float32 [32, 131072], P(None, ('col', 'vol')), may hold values from -6 to 6
- source: float32 [32, 128, 64, 512], P(None, 'row', 'col', 'vol'), may hold values from -6 to 6
- class_index: int32 [128, 64, 512], P('row', 'col', 'vol'), may hold values from 0 to 15
- class_values: float32 [16], replicated, may hold values from 0.2 to 5
- trace_count: int32 [16, 32], P('row'), may hold values from 1 to 16, 128 in all within a row
- trace_cell: int32 [16, 32, 16], P('row'), may hold values from 0 to 8191
Outputs:
- density_out: float32 [32, 131072], P(None, ('col', 'vol'))
- volume_out: float32 [32, 128, 64, 512], P(None, 'row', 'col', 'vol')
Inputs may be any that keep to these rules, and one draw needn't show every extreme that they name: `trace_count`: in each row r, the counts of the 32 blocks are 1 or more and sum to 128, so that every target of row tile r has exactly one live slot; the largest count of each row is 16. `trace_cell`: only the first trace_count[r, j] slots of block j are read; two slots may hit one cell.
All inputs are finite; a program needn't handle non-finite values.
Results may differ from a plain program's by a relative error of at most 0.00035.
Values may be sent and summed in bfloat16 or wider, within the bound.
A program may use at most 128 MiB of HBM per device.

v0:
```python
import functools
import math

import jax
import jax.numpy as jnp
from jax import lax
from jax.experimental import pallas as pl
from jax.experimental.pallas import tpu as pltpu
from jax.sharding import PartitionSpec as P

SWEEPS = 4
OUTER = 2
MASS_TERM = 0.1
RELAXATION = 0.5
SPECTRUM_LOW = 0.1
SPECTRUM_HIGH = 2.0
MESH = pl.DeviceIdType.MESH
F32 = jnp.float32
BF16 = jnp.bfloat16
GROUP = 16
NT = (((1,), (1,)), ((), ()))


def relax_factors(count):
    middle = (SPECTRUM_HIGH + SPECTRUM_LOW) / 2.0
    spread = (SPECTRUM_HIGH - SPECTRUM_LOW) / 2.0
    return [
        1.0 / (middle + spread * math.cos(math.pi * (2 * order + 1) / (2 * count)))
        for order in range(count)
    ]


def kernel(
    sizes,
    panel, density, source, class_index, class_values, target_of, cell_of,
    density_out, volume_out,
    select, hot, spots, conduct, inverse, base, field, xlo, xhi, ylo, yhi, zlo, zhi,
    yface, zface, zmix, slot, picked, psend, pbuf, fsend, fbuf, fall, strip, dsend, rbuf, osend,
    halo_send, halo_recv, phase_send, phase_recv,
):
    n_row, n_col, n_vol = sizes
    blocks = n_col * n_vol
    columns = blocks // 8
    share = density.shape[1] // n_row
    lead = source.shape[0]
    high = lead // 8
    factors = relax_factors(SWEEPS)
    row = lax.axis_index("row")
    col = lax.axis_index("col")
    vol = lax.axis_index("vol")
    me = col * n_vol + vol

    def block_id(j):
        return {"col": j // n_vol, "vol": j % n_vol}

    def block_peer(d):
        return lax.rem(me + d, blocks)

    def row_peer(d):
        return lax.rem(row + d, n_row)

    barrier = pltpu.get_barrier_semaphore()

    @pl.loop(1, blocks)
    def _(d):
        pl.semaphore_signal(barrier, inc=1, device_id=block_id(block_peer(d)), device_id_type=MESH)

    @pl.loop(1, n_row)
    def _(d):
        pl.semaphore_signal(barrier, inc=1, device_id={"row": row_peer(d)}, device_id_type=MESH)

    def remote(src, dst, send, recv, device):
        return pltpu.make_async_remote_copy(
            src_ref=src, dst_ref=dst, send_sem=send, recv_sem=recv,
            device_id=device, device_id_type=MESH,
        )

    def whole(ref, phase):
        return remote(ref, ref, phase_send.at[phase], phase_recv.at[phase], {"row": row})

    sub = lax.broadcasted_iota(jnp.int32, (8, 128), 0)
    lane = lax.broadcasted_iota(jnp.int32, (8, 128), 1)
    group = lane // GROUP

    rows_t = lax.broadcasted_iota(jnp.int32, select.shape, 0)
    select[...] = jnp.where(rows_t == target_of[0:1, :], 1.0, 0.0).astype(F32)
    cells = cell_of[0:1, :]
    hot_z = lax.broadcasted_iota(jnp.int32, hot.shape, 0)
    hot[...] = jnp.where(hot_z == cells % 128, 1.0, 0.0).astype(F32)
    spot_rows = lax.broadcasted_iota(jnp.int32, (64, 128), 0)
    spot_lane = lax.broadcasted_iota(jnp.int32, (64, 128), 1)
    part = lax.rem(spot_lane // GROUP - lax.rem(me, 8) + 8, 8)
    hit = (spot_rows == cells // 128) & (cells >= 0)
    for h in range(high):
        spots[h] = jnp.where(hit & (part == h), 1.0, 0.0).astype(F32)
    cls = class_index[...]
    value = jnp.zeros(cls.shape, F32)
    for k in range(class_values.shape[0]):
        value = jnp.where(cls == k, class_values[k], value)
    diagonal = MASS_TERM + 6.0 * value
    conduct[...] = value / diagonal
    inverse[...] = 1.0 / diagonal

    exchanges = xlo.shape[0]

    def clear(ref):
        @pl.loop(0, exchanges)
        def _(k):
            ref[k] = jnp.zeros(ref.shape[1:], F32)

    for here, edge, ref in (
        (row, 0, xlo), (row, n_row - 1, xhi), (col, 0, ylo),
        (col, n_col - 1, yhi), (vol, 0, zlo), (vol, n_vol - 1, zhi),
    ):
        @pl.when(here == edge)
        def _(ref=ref):
            clear(ref)

    def send_potential(it, chunk):
        partial = jnp.zeros((lead, panel.shape[0]), F32)
        for k in range(n_row):
            partial += lax.dot_general(
                chunk(k), panel[:, k * share : (k + 1) * share], NT, preferred_element_type=F32
            )
        chosen = jnp.dot(
            partial, select[...], precision=lax.Precision.HIGHEST, preferred_element_type=F32
        )
        for g in range(columns):
            turned = [
                pltpu.roll(
                    chosen[8 * h : 8 * h + 8, 128 * g : 128 * g + 128], (GROUP * h) % 128, 1
                )
                for h in range(high)
            ]
            for d in range(8):
                tile = jnp.zeros((8, 128), F32)
                for h in range(high):
                    tile = jnp.where(group == (d + h) % 8, turned[h], tile)
                psend[it, g * 8 + d] = tile
        if it == 0:
            pl.semaphore_wait(barrier, blocks - 1 + n_row - 1)
        pbuf[it, me] = psend[it, me]

        @pl.loop(1, blocks)
        def _(d):
            j = block_peer(d)
            remote(
                psend.at[it, j], pbuf.at[it, me], phase_send.at[it], phase_recv.at[it], block_id(j)
            ).start()

    def right_side(it):
        whole(pbuf.at[it, pl.ds(0, blocks - 1)], it).wait_recv()
        total = pbuf[it, 0]
        for j in range(1, blocks):
            total += pbuf[it, j]
        slot[...] = total

        def build(low, carry):
            for h in range(high):
                spread = slot[pl.ds(low, 1), :] * spots[h]
                added = lax.dot_general(
                    spread, hot[...], NT, precision=lax.Precision.HIGHEST,
                    preferred_element_type=F32,
                )
                e = h * 8 + low
                base[e] = (source[e] + added) * inverse[...]
            return carry

        lax.fori_loop(0, 8, build, 0)

    def faces(slot_index, e, new, packed):
        out = []
        for x in range(8):
            moved = pltpu.roll(new[x], lax.rem(2 * e, 128), 1)
            ours = (lane == 2 * e) | (lane == lax.rem(2 * e + 127, 128))
            out.append(jnp.where(ours, moved, packed[x]))
        yface[slot_index, 0, e] = field[slot_index, e, pl.ds(0, 8, stride=8), :]
        yface[slot_index, 1, e] = field[slot_index, e, pl.ds(7, 8, stride=8), :]
        return out

    def first_sweep(out_index, factor):
        def step(e, packed):
            new = [factor * base[e, 8 * x : 8 * x + 8, :] for x in range(8)]
            for x in range(8):
                field[out_index, e, 8 * x : 8 * x + 8, :] = new[x]
            return faces(out_index, e, new, packed)

        packed = lax.fori_loop(0, lead, step, [jnp.zeros((8, 128), F32)] * 8)
        for x in range(8):
            zface[out_index, x] = packed[x]

    def halo_copies(k):
        return (
            (row < n_row - 1, remote(field.at[k, :, pl.ds(56, 8), :], xlo.at[k], halo_send.at[k, 0], halo_recv.at[k, 0], {"row": row + 1})),
            (row > 0, remote(field.at[k, :, pl.ds(0, 8), :], xhi.at[k], halo_send.at[k, 1], halo_recv.at[k, 1], {"row": row - 1})),
            (col < n_col - 1, remote(yface.at[k, 1], ylo.at[k], halo_send.at[k, 2], halo_recv.at[k, 2], {"col": col + 1})),
            (col > 0, remote(yface.at[k, 0], yhi.at[k], halo_send.at[k, 3], halo_recv.at[k, 3], {"col": col - 1})),
            (vol < n_vol - 1, remote(zface.at[k], zlo.at[k], halo_send.at[k, 4], halo_recv.at[k, 4], {"vol": vol + 1})),
            (vol > 0, remote(zface.at[k], zhi.at[k], halo_send.at[k, 5], halo_recv.at[k, 5], {"vol": vol - 1})),
        )

    arrives = (row > 0, row < n_row - 1, col > 0, col < n_col - 1, vol > 0, vol < n_vol - 1)

    def halo_start(k):
        copies = halo_copies(k)
        for i in (4, 5, 0, 1, 2, 3):
            @pl.when(copies[i][0])
            def _(copy=copies[i][1]):
                copy.start()

    def halo_wait(k):
        for i, (_, copy) in enumerate(halo_copies(k)):
            @pl.when(arrives[i])
            def _(copy=copy):
                copy.wait_recv()

    def halo_sent(k):
        for go, copy in halo_copies(k):
            @pl.when(go)
            def _(copy=copy):
                copy.wait_send()

    def sweep(k, factor, last):
        halo_wait(k)
        odd = lax.rem(lane, 2) == 1
        for x in range(8):
            zmix[x] = jnp.where(odd, pltpu.roll(zlo[k, x], 2, 1), zhi[k, x])

        def step(e, packed):
            old = [field[k, e, 8 * x : 8 * x + 8, :] for x in range(8)]
            new = []
            turn = lax.rem(127 - 2 * e + 128, 128)
            for x in range(8):
                c = old[x]
                below = xlo[k, e] if x == 0 else old[x - 1]
                above = xhi[k, e] if x == 7 else old[x + 1]
                left = jnp.where(sub == 0, ylo[k, e, x : x + 1, :], pltpu.roll(c, 1, 0))
                right = jnp.where(sub == 7, yhi[k, e, x : x + 1, :], pltpu.roll(c, 7, 0))
                ends = pltpu.roll(zmix[x], turn, 1)
                front = jnp.where(lane == 0, ends, pltpu.roll(c, 1, 1))
                back = jnp.where(lane == 127, ends, pltpu.roll(c, 127, 1))
                around = (below + above) + (left + right) + (front + back)
                span = slice(8 * x, 8 * x + 8)
                n = (1.0 - factor) * c + factor * (base[e, span, :] + conduct[span, :] * around)
                if last:
                    volume_out[e, span, :] = n
                else:
                    field[k + 1, e, span, :] = n
                new.append(n)
            if last:
                return packed
            return faces(k + 1, e, new, packed)

        if last:
            lax.fori_loop(0, lead, step, 0)
        else:
            packed = lax.fori_loop(0, lead, step, [jnp.zeros((8, 128), F32)] * 8)
            for x in range(8):
                zface[k + 1, x] = packed[x]

    def send_flux(it, read):
        def pick(low, carry):
            total = jnp.zeros((8, 128), F32)
            for h in range(high):
                seen = jnp.dot(
                    read(h * 8 + low), hot[...], precision=lax.Precision.HIGHEST,
                    preferred_element_type=F32,
                ) * spots[h]
                for x in range(8):
                    total += seen[8 * x : 8 * x + 8, :]
            picked[pl.ds(low, 1), :] = jnp.sum(total, axis=0, keepdims=True)
            return carry

        lax.fori_loop(0, 8, pick, 0)
        flux = picked[...] - slot[...]
        fsend[it] = flux
        fbuf[it, me] = flux

        @pl.loop(1, blocks)
        def _(d):
            remote(
                fsend.at[it], fbuf.at[it, me], phase_send.at[2 + it], phase_recv.at[2 + it],
                block_id(block_peer(d)),
            ).start()

    def spread_flux(it):
        whole(fbuf.at[it, pl.ds(0, blocks - 1)], 2 + it).wait_recv()
        dense = jnp.zeros((lead, panel.shape[0]), F32)
        for g in range(columns):
            parts = []
            for h in range(high):
                mixed = fbuf[it, g * 8]
                for d in range(1, 8):
                    mixed = jnp.where(group == (d + h) % 8, fbuf[it, g * 8 + d], mixed)
                parts.append(pltpu.roll(mixed, (128 - GROUP * h) % 128, 1))
            block = jnp.concatenate(parts, axis=0).astype(BF16)
            dense += lax.dot_general(
                block, select[:, 128 * g : 128 * g + 128].astype(BF16), NT,
                preferred_element_type=F32,
            )
        fall[it, row] = dense.astype(BF16)

        @pl.loop(1, n_row)
        def _(d):
            remote(
                fall.at[it, row], fall.at[it, row], phase_send.at[4 + it], phase_recv.at[4 + it],
                {"row": row_peer(d)},
            ).start()

    def panel_copy(d):
        r = row_peer(d)
        return remote(
            panel.at[:, pl.ds(pl.multiple_of(r * share, share), share)], strip.at[row],
            phase_send.at[6], phase_recv.at[6], {"row": r},
        )

    def send_panel(first, count):
        @pl.loop(first, min(first + count, n_row))
        def _(d):
            panel_copy(d).start()

    def new_share(it, old):
        whole(fall.at[it, pl.ds(0, n_row - 1)], 4 + it).wait_recv()
        if it == 0:
            whole(strip.at[pl.ds(0, n_row - 1)], 6).wait_recv()
        update = jnp.zeros((lead, share), F32)
        for r in range(n_row):
            update += jnp.dot(fall[it, r], strip[r], preferred_element_type=F32)
        return old + RELAXATION * update

    own = pl.ds(pl.multiple_of(row * share, share), share)

    send_potential(0, lambda k: density[:, k * share : (k + 1) * share].astype(BF16))
    strip[row] = panel[:, own]
    send_panel(1, 4)
    right_side(0)
    first_sweep(0, factors[0])
    halo_start(0)
    send_panel(5, 4)
    sweep(0, factors[1], False)
    halo_start(1)
    send_panel(9, 4)
    sweep(1, factors[2], False)
    halo_start(2)
    send_panel(13, n_row)
    sweep(2, factors[3], False)
    send_flux(0, lambda e: field[3, e])
    halo_start(3)
    spread_flux(0)
    state = new_share(0, density[:, own])
    osend[0] = state
    rounded = state.astype(BF16)
    dsend[...] = rounded
    rbuf[row] = rounded

    @pl.loop(1, n_row)
    def _(d):
        remote(
            dsend, rbuf.at[row], phase_send.at[7], phase_recv.at[7], {"row": row_peer(d)}
        ).start()

    whole(rbuf.at[pl.ds(0, n_row - 1)], 7).wait_recv()

    send_potential(1, lambda k: rbuf[k])
    right_side(1)
    sweep(3, factors[0], False)
    halo_start(4)
    sweep(4, factors[1], False)
    halo_start(5)
    sweep(5, factors[2], False)
    halo_start(6)
    sweep(6, factors[3], True)
    send_flux(1, lambda e: volume_out[e])
    spread_flux(1)
    state = new_share(1, osend[0])
    osend[1] = state
    density_out[:, own] = state

    @pl.loop(1, n_row)
    def _(d):
        remote(
            osend.at[1], density_out.at[:, own], phase_send.at[8], phase_recv.at[8],
            {"row": row_peer(d)},
        ).start()

    whole(density_out.at[:, pl.ds(0, (n_row - 1) * share)], 8).wait_recv()

    for it in range(OUTER):
        whole(pbuf.at[it, pl.ds(0, blocks - 1)], it).wait_send()
        whole(fbuf.at[it, pl.ds(0, blocks - 1)], 2 + it).wait_send()
        whole(fall.at[it, pl.ds(0, n_row - 1)], 4 + it).wait_send()
    whole(strip.at[pl.ds(0, n_row - 1)], 6).wait_send()
    whole(rbuf.at[pl.ds(0, n_row - 1)], 7).wait_send()
    whole(density_out.at[:, pl.ds(0, (n_row - 1) * share)], 8).wait_send()
    for k in range(exchanges):
        halo_sent(k)


def local(panel, density, source, class_index, class_values, trace_count, trace_cell):
    sizes = (lax.axis_size("row"), lax.axis_size("col"), lax.axis_size("vol"))
    n_row, n_col, n_vol = sizes
    blocks = n_col * n_vol
    lead = source.shape[0]
    targets, nodes = panel.shape
    share = nodes // n_row
    slots = trace_cell.shape[2]
    counts = trace_count[0]
    offsets = jnp.cumsum(counts) - counts
    slot_ids = jnp.arange(slots, dtype=jnp.int32)
    live = slot_ids[None, :] < counts[:, None]
    target_of = jnp.where(live, offsets[:, None] + slot_ids[None, :], -1)
    target_of = jnp.broadcast_to(target_of.reshape(1, blocks * slots), (8, blocks * slots))
    block_index = lax.axis_index(("col", "vol"))
    cells = jnp.where(live, trace_cell[0], -1)
    cells = lax.dynamic_index_in_dim(cells, block_index, keepdims=False)
    cell_of = jnp.broadcast_to(cells[None, None, :], (8, 8, slots)).reshape(8, 8 * slots)
    exchanges = SWEEPS * OUTER - 1
    vmem = lambda shape, kind=F32: pltpu.VMEM(shape, kind)
    dma = pltpu.SemaphoreType.DMA
    density_out, volume = pl.pallas_call(
        functools.partial(kernel, sizes),
        out_shape=(
            jax.ShapeDtypeStruct(density.shape, F32),
            jax.ShapeDtypeStruct((lead, 64, 128), F32),
        ),
        in_specs=[
            pl.BlockSpec(memory_space=pltpu.VMEM),
            pl.BlockSpec(memory_space=pltpu.VMEM),
            pl.BlockSpec(memory_space=pltpu.VMEM),
            pl.BlockSpec(memory_space=pltpu.VMEM),
            pl.BlockSpec(memory_space=pltpu.SMEM),
            pl.BlockSpec(memory_space=pltpu.VMEM),
            pl.BlockSpec(memory_space=pltpu.VMEM),
        ],
        out_specs=(
            pl.BlockSpec(memory_space=pltpu.VMEM),
            pl.BlockSpec(memory_space=pltpu.VMEM),
        ),
        scratch_shapes=[
            vmem((targets, blocks * slots)),
            vmem((128, 128)),
            vmem((lead // 8, 64, 128)),
            vmem((64, 128)),
            vmem((64, 128)),
            vmem((lead, 64, 128)),
            vmem((exchanges, lead, 64, 128)),
            vmem((exchanges, lead, 8, 128)),
            vmem((exchanges, lead, 8, 128)),
            vmem((exchanges, lead, 8, 128)),
            vmem((exchanges, lead, 8, 128)),
            vmem((exchanges, 8, 8, 128)),
            vmem((exchanges, 8, 8, 128)),
            vmem((exchanges, 2, lead, 8, 128)),
            vmem((exchanges, 8, 8, 128)),
            vmem((8, 8, 128)),
            vmem((8, 128)),
            vmem((8, 128)),
            vmem((OUTER, blocks, 8, 128)),
            vmem((OUTER, blocks, 8, 128)),
            vmem((OUTER, 8, 128)),
            vmem((OUTER, blocks, 8, 128)),
            vmem((OUTER, n_row, lead, targets), BF16),
            vmem((n_row, targets, share), BF16),
            vmem((lead, share), BF16),
            vmem((n_row, lead, share), BF16),
            vmem((OUTER, lead, share)),
            dma((exchanges, 6)),
            dma((exchanges, 6)),
            dma((9,)),
            dma((9,)),
        ],
        compiler_params=pltpu.CompilerParams(
            collective_id=0, has_side_effects=True, vmem_limit_bytes=56 * 1024 * 1024
        ),
    )(
        panel,
        density,
        source.reshape(lead, 64, 128),
        class_index.reshape(64, 128),
        class_values,
        target_of,
        cell_of,
    )
    return density_out, volume.reshape(source.shape)


def solution(mesh):
    placed = (
        P("row", ("col", "vol")),
        P(None, ("col", "vol")),
        P(None, "row", "col", "vol"),
        P("row", "col", "vol"),
        P(),
        P("row", None),
        P("row", None, None),
    )
    return jax.shard_map(
        local,
        mesh=mesh,
        in_specs=placed,
        out_specs=(P(None, ("col", "vol")), P(None, "row", "col", "vol")),
        check_vma=False,
    )
```

profile of v0, /device:TPU:56, one launch (start us, length us, event | category | flops | bytes accessed | tf_op | source)
XLA Modules:
  0.0 188.9 jit_solution(5089565781939857104)
XLA Ops:
  0.6 0.0 copy-start.1
  0.6 0.0 copy-start.2
  0.7 0.7 copy-done.2
  1.3 0.0 copy-done.1
  1.3 0.2 fusion
  1.5 0.1 broadcast_in_dim.29
  1.6 0.6 broadcast_in_dim.30.cell_of
  2.2 0.1 copy.10
  2.3 0.1 reduce-window.8
  2.4 0.1 reduce
  2.5 0.1 copy.11
  2.6 0.1 select_n.19
  2.6 0.6 broadcast_in_dim.26.target_of
  3.3 182.7 %shard_map.86 = (f32[32,4096]{1,0:T(8,128)}, f32[32,64,128]{2,1,0:T(8,128)}) custom-call(bf16[128,4096]{1,0:T(8,128)(2,1)} %panel.1, f32[32,4096]{1,0:T(8,128)} %density.1, f32[32,64,128]{2,1,0:T(8,128)} %bitcast.7, s32[64,128]{1,0:T(8,128)} %bitcast.9, f32[16]{0:T(128)} %class_values.1, s32[8,512]{1,0:T(8,128)} %broadcast_in_dim.26.target_of, ...), custom_call_target="tpu_custom_call" | custom-call | tf_op jit(solution)/shard_map/pallas_call | solution.py:420
  186.0 0.0 copy-start
  186.0 2.0 %copy.14 = f32[32,4096]{1,0:T(8,128)} copy(f32[32,4096]{1,0:T(8,128)} %get-tuple-element.8) | data formatting | bytes 1048576
  187.9 0.0 copy-done
  187.9 1.0 copy.15
  (4 shorter events, 0.0 us)
Async XLA Ops:
  0.6 0.7 copy-start.1
  0.6 0.7 copy-start.2
  186.0 2.0 %copy-start = (f32[32,64,128]{2,1,0:T(8,128)S(1)}, f32[32,64,128]{2,1,0:T(8,128)}, u32[]{:S(2)}) copy-start(f32[32,64,128]{2,1,0:T(8,128)} %get-tuple-element.5) | copy-start | bytes 3145732
where the time goes:
time: 190 us; the launch traced here: 189 us
  Pallas kernels  183 us (96%)
  local copies, waits for them, and re-layouts  5.16 us (3%)
    pallas_call x1, Pallas kernels, local(): pl.pallas_call(functools.partial(kernel, sizes), out_shape=(jax.ShapeDtyp...  183 us

commit v1 on v0

v1 whole, which is shorter than its diff:
```python
import functools
import math

import jax
import jax.numpy as jnp
from jax import lax
from jax.experimental import pallas as pl
from jax.experimental.pallas import tpu as pltpu
from jax.sharding import PartitionSpec as P

SWEEPS = 4
OUTER = 2
MASS_TERM = 0.1
RELAXATION = 0.5
SPECTRUM_LOW = 0.1
SPECTRUM_HIGH = 2.0
MESH = pl.DeviceIdType.MESH
F32 = jnp.float32
BF16 = jnp.bfloat16
NT = (((1,), (1,)), ((), ()))
TN = (((0,), (0,)), ((), ()))
SLOTS = 16
TURN = 4
SPANS = tuple(slice(8 * b, 8 * b + 8) for b in range(4))


def relax_factors(count):
    middle = (SPECTRUM_HIGH + SPECTRUM_LOW) / 2.0
    spread = (SPECTRUM_HIGH - SPECTRUM_LOW) / 2.0
    return [
        1.0 / (middle + spread * math.cos(math.pi * (2 * order + 1) / (2 * count)))
        for order in range(count)
    ]


def kernel(
    sizes,
    panel, density, source, class_index, class_values, trace_count, trace_cell,
    density_out, volume_out,
    select, hits, conduct, inverse, inner, middle, base, field, zface, zlo, zhi, zrow, zmix,
    turned, slot, picked, psend, pbuf, fsend, fbuf, fall, strip, rbuf, osend,
    halo_send, halo_recv, phase_send, phase_recv,
):
    n_row, n_col, n_vol = sizes
    blocks = n_col * n_vol
    share = density.shape[1] // n_row
    lead = density.shape[0]
    factors = relax_factors(SWEEPS)
    row = lax.axis_index("row")
    col = lax.axis_index("col")
    vol = lax.axis_index("vol")
    me = col * n_vol + vol

    def block_id(j):
        return {"col": j // n_vol, "vol": j % n_vol}

    def block_peer(d):
        return lax.rem(me + d, blocks)

    def row_peer(d):
        return lax.rem(row + d, n_row)

    barrier = pltpu.get_barrier_semaphore()

    @pl.loop(1, blocks)
    def _(d):
        pl.semaphore_signal(barrier, inc=1, device_id=block_id(block_peer(d)), device_id_type=MESH)

    @pl.loop(1, n_row)
    def _(d):
        pl.semaphore_signal(barrier, inc=1, device_id={"row": row_peer(d)}, device_id_type=MESH)

    def remote(src, dst, send, recv, device):
        return pltpu.make_async_remote_copy(
            src_ref=src, dst_ref=dst, send_sem=send, recv_sem=recv,
            device_id=device, device_id_type=MESH,
        )

    def whole(ref, phase):
        return remote(ref, ref, phase_send.at[phase], phase_recv.at[phase], {"row": row})

    sub = lax.broadcasted_iota(jnp.int32, (8, 128), 0)
    lane = lax.broadcasted_iota(jnp.int32, (8, 128), 1)
    group = lane // 32
    exchanges = field.shape[0]

    def pieces(x):
        first = x.astype(BF16)
        rest = x - first.astype(F32)
        second = rest.astype(BF16)
        third = (rest - second.astype(F32)).astype(BF16)
        return first, second, third

    offset = jnp.int32(0)
    marks = []
    for j in range(blocks):
        count = trace_count[0, j]
        marks.append((offset, count))
        offset = offset + count
    for p in range(2):
        for j in range(0, blocks, 2):
            both = []
            for start, count in marks[j : j + 2]:
                s = sub + 8 * p
                both.append(jnp.where((lane == s + start) & (s < count), 1.0, 0.0).astype(F32))
            at = p * blocks * 8 + j * 8
            select[at : at + 16, :] = jnp.concatenate(both, axis=0).astype(BF16)

    def quarters(tiles):
        a = list(tiles)
        grp = lax.broadcasted_iota(jnp.int32, a[0].shape, 1) // 32
        for step in (2, 1):
            out = list(a)
            for i in range(4):
                if i & step == 0:
                    j = i | step
                    shift = 32 * step
                    keep = (grp & step) == 0
                    out[i] = jnp.where(keep, a[i], pltpu.roll(a[j], shift, 1))
                    out[j] = jnp.where(keep, pltpu.roll(a[i], 128 - shift, 1), a[j])
            a = out
        return a

    def to_inner(rows, write):
        @pl.loop(0, 16, unroll=TURN)
        def _(i):
            x, y = i // 2, (i % 2) * 4
            stacked = jnp.concatenate([rows(x, y + q) for q in range(4)], axis=0)
            flipped = jnp.transpose(stacked)
            for q, tile in enumerate(quarters([flipped[32 * q : 32 * q + 32, :] for q in range(4)])):
                write(x, y + q, tile)

    cls = class_index[...]
    value = jnp.zeros(cls.shape, F32)
    for k in range(class_values.shape[0]):
        value = jnp.where(cls == k, class_values[k], value)
    turned[...] = value

    def coefficients(x, y, tile):
        inv = 1.0 / (MASS_TERM + 6.0 * tile)
        inverse[x, y] = inv
        conduct[x, y] = tile * inv

    def prepare():
        to_inner(
            lambda x, y: jnp.broadcast_to(turned[pl.ds(x * 8 + y, 1), :], (lead, 128)), coefficients
        )

    def send_potential(it, chunk):
        partial = jnp.zeros((panel.shape[0], 128), F32)
        for k in range(n_row):
            part = chunk(k)
            partial += lax.dot_general(
                panel[:, k * share : (k + 1) * share],
                jnp.concatenate([part] * (128 // lead), axis=0),
                NT, preferred_element_type=F32,
            )
        chosen = jnp.zeros((select.shape[0], 128), F32)
        for piece in pieces(partial):
            chosen += jnp.dot(select[...], piece, preferred_element_type=F32)
        half = blocks * 8
        for j in range(blocks):
            psend[it, j] = jnp.where(
                group % 2 == 0, chosen[8 * j : 8 * j + 8, :],
                chosen[half + 8 * j : half + 8 * j + 8, :],
            )
        if it == 0:
            prepare()
            pl.semaphore_wait(barrier, blocks - 1 + n_row - 1)
        pbuf[it, me] = psend[it, me]

        @pl.loop(1, blocks)
        def _(d):
            j = block_peer(d)
            remote(
                psend.at[it, j], pbuf.at[it, me], phase_send.at[it], phase_recv.at[it], block_id(j)
            ).start()

    def panel_copy(d):
        r = row_peer(d)
        return remote(
            panel.at[:, pl.ds(pl.multiple_of(r * share, share), share)], strip.at[row],
            phase_send.at[6], phase_recv.at[6], {"row": r},
        )

    def send_panel(first, count):
        @pl.loop(first, min(first + count, n_row))
        def _(d):
            panel_copy(d).start()

    own = pl.ds(pl.multiple_of(row * share, share), share)
    send_potential(0, lambda k: density[:, k * share : (k + 1) * share].astype(BF16))
    strip[row] = panel[:, own]
    send_panel(1, 4)

    own_count = trace_count[0, me]
    cells, spot = [], jnp.full((8, 128), -1, jnp.int32)
    quarter = [jnp.full((8, 128), -1, jnp.int32) for _ in range(2)]
    for s in range(SLOTS):
        cell = jnp.where(s < own_count, trace_cell[0, me, s], -1)
        place = (cell >> 7) * 32 + (cell & 31)
        spot = jnp.where(lane % SLOTS == s, jnp.where(cell >= 0, place, -1), spot)
        fourth = jnp.where(cell >= 0, (cell >> 5) & 3, -1)
        quarter[s // 8] = jnp.where(sub == s % 8, fourth, quarter[s // 8])
        cells.append(jnp.maximum(place, 0))
    mine = [jnp.where(quarter[p] == group, 1.0, 0.0).astype(F32) for p in range(2)]
    spot = jnp.where(lane < 3 * SLOTS, spot, -1)

    @pl.loop(0, 128)
    def _(i):
        at = pl.multiple_of(i * 16, 16)
        here = jnp.concatenate([sub, sub + 8], axis=0) + at
        wide = jnp.concatenate([spot, spot], axis=0)
        hits[pl.ds(at, 16), :] = jnp.where(here == wide, 1.0, 0.0).astype(BF16)

    def keep_source(x, y, tile):
        inner[x, y] = tile

    to_inner(lambda x, y: source[pl.ds(x * 8 + y, lead, stride=64), :], keep_source)

    def clear(write):
        @pl.loop(0, exchanges)
        def _(k):
            write(k)

    def clear_x(k, x):
        field[k, x] = jnp.zeros(field.shape[2:], F32)

    def clear_y(k, y):
        @pl.loop(0, 10)
        def _(x):
            field[k, x, y] = jnp.zeros(field.shape[3:], F32)

    def clear_z(ref, k):
        ref[k] = jnp.zeros(ref.shape[1:], F32)

    for here, edge, write in (
        (row, 0, lambda k: clear_x(k, 0)), (row, n_row - 1, lambda k: clear_x(k, 9)),
        (col, 0, lambda k: clear_y(k, 0)), (col, n_col - 1, lambda k: clear_y(k, 9)),
        (vol, 0, lambda k: clear_z(zlo, k)), (vol, n_vol - 1, lambda k: clear_z(zhi, k)),
    ):
        @pl.when(here == edge)
        def _(write=write):
            clear(write)

    def right_side(it):
        whole(pbuf.at[it, pl.ds(0, blocks - 1)], it).wait_recv()
        total = pbuf[it, 0]
        for j in range(1, blocks):
            total += pbuf[it, j]
        swapped = pltpu.roll(total, 32, 1)
        even = group % 2 == 0
        parts = [jnp.where(even, total, swapped), jnp.where(even, swapped, total)]
        for p in range(2):
            slot[p] = parts[p]
        placed = jnp.concatenate([parts[p] * mine[p] for p in range(2)], axis=0)
        values = jnp.concatenate(
            list(pieces(placed)) + [jnp.zeros((128 - 3 * SLOTS, 128), BF16)], axis=0
        )

        @pl.loop(0, 8)
        def _(x):
            at = pl.multiple_of(x * 256, 256)
            added = jnp.dot(hits[pl.ds(at, 256), :], values, preferred_element_type=F32)
            for y in range(8):
                base[x, y] = (inner[x, y] + added[32 * y : 32 * y + 32, :]) * inverse[x, y]

    def keep(k, x, y, new, packed):
        low, top = packed
        for b in range(4):
            field[k, x + 1, y + 1, SPANS[b], :] = new[b]
        low = jnp.where(sub == y, pltpu.roll(new[0], y, 0) if y else new[0], low)
        top = jnp.where(sub == y, pltpu.roll(new[3], y + 1, 0) if y < 7 else new[3], top)
        return low, top

    def pack_rows(k):
        for side, edge in ((0, 0), (1, 3)):
            for b in range(2):
                packed = jnp.zeros((8, 128), F32)
                for i in range(4):
                    moved = zrow[k, side, 4 * b + i]
                    if i != edge:
                        moved = pltpu.roll(moved, (32 * (i - edge)) % 128, 1)
                    packed = jnp.where(group == i, moved, packed)
                zface[k, side, b] = packed

    def first_sweep(k, factor):
        @pl.loop(0, 8)
        def _(x):
            packed = (jnp.zeros((8, 128), F32),) * 2
            for y in range(8):
                new = [factor * base[x, y, SPANS[b], :] for b in range(4)]
                packed = keep(k, x, y, new, packed)
            zrow[k, 0, x], zrow[k, 1, x] = packed

        pack_rows(k)

    def halo_copies(k):
        pairs = (
            (row < n_row - 1, field.at[k, 8, pl.ds(1, 8)], field.at[k, 0, pl.ds(1, 8)], {"row": row + 1}),
            (row > 0, field.at[k, 1, pl.ds(1, 8)], field.at[k, 9, pl.ds(1, 8)], {"row": row - 1}),
            (col < n_col - 1, field.at[k, pl.ds(1, 8), 8], field.at[k, pl.ds(1, 8), 0], {"col": col + 1}),
            (col > 0, field.at[k, pl.ds(1, 8), 1], field.at[k, pl.ds(1, 8), 9], {"col": col - 1}),
            (vol < n_vol - 1, zface.at[k, 1], zlo.at[k], {"vol": vol + 1}),
            (vol > 0, zface.at[k, 0], zhi.at[k], {"vol": vol - 1}),
        )
        return [
            (go, remote(src, dst, halo_send.at[k, i], halo_recv.at[k, i], device))
            for i, (go, src, dst, device) in enumerate(pairs)
        ]

    arrives = (row > 0, row < n_row - 1, col > 0, col < n_col - 1, vol > 0, vol < n_vol - 1)

    def halo_start(k):
        copies = halo_copies(k)
        for i in (4, 5, 0, 1, 2, 3):
            @pl.when(copies[i][0])
            def _(copy=copies[i][1]):
                copy.start()

    def halo_wait(k):
        for i, (_, copy) in enumerate(halo_copies(k)):
            @pl.when(arrives[i])
            def _(copy=copy):
                copy.wait_recv()

    def halo_sent(k):
        for go, copy in halo_copies(k):
            @pl.when(go)
            def _(copy=copy):
                copy.wait_send()

    def sweep(k, factor, last, seen=None):
        halo_wait(k)
        for x in range(8):
            b, i = x // 4, x % 4
            low, top = zlo[k, b], zhi[k, b]
            low = pltpu.roll(low, 32 * (3 - i), 1) if i < 3 else low
            top = pltpu.roll(top, (128 - 32 * i) % 128, 1) if i else top
            zmix[0, x] = pltpu.roll(jnp.where(group == 3, low, zrow[k, 1, x]), 32, 1)
            zmix[1, x] = pltpu.roll(jnp.where(group == 0, top, zrow[k, 0, x]), 96, 1)

        @pl.loop(0, 8)
        def _(x):
            packed = (jnp.zeros((8, 128), F32),) * 2
            for y in range(8):
                c = [field[k, x + 1, y + 1, SPANS[b], :] for b in range(4)]
                ups = [pltpu.roll(v, 1, 0) for v in c]
                downs = [pltpu.roll(v, 7, 0) for v in c]
                new = []
                for b in range(4):
                    before = zmix[0, x, y : y + 1, :] if b == 0 else ups[b - 1]
                    after = zmix[1, x, y : y + 1, :] if b == 3 else downs[b + 1]
                    up = jnp.where(sub == 0, before, ups[b])
                    down = jnp.where(sub == 7, after, downs[b])
                    sp = SPANS[b]
                    around = (
                        (field[k, x, y + 1, sp, :] + field[k, x + 2, y + 1, sp, :])
                        + (field[k, x + 1, y, sp, :] + field[k, x + 1, y + 2, sp, :])
                        + (up + down)
                    )
                    new.append(
                        (1.0 - factor) * c[b]
                        + factor * (base[x, y, sp, :] + conduct[x, y, sp, :] * around)
                    )
                if seen is not None:
                    for b in range(4):
                        seen[x, y, SPANS[b], :] = new[b]
                if not last:
                    packed = keep(k + 1, x, y, new, packed)
            if not last:
                zrow[k + 1, 0, x], zrow[k + 1, 1, x] = packed

        if not last:
            pack_rows(k + 1)

    def send_flux(it, ref):
        for s in range(SLOTS):
            place = cells[s]
            picked[s : s + 1, :] = ref[
                place >> 8, (place >> 5) & 7, pl.ds(place & 31, 1), :
            ]
        fluxes = []
        for p in range(2):
            seen = picked[8 * p : 8 * p + 8, :] * mine[p]
            seen = seen + pltpu.roll(seen, 64, 1)
            seen = seen + pltpu.roll(seen, 32, 1)
            fluxes.append(seen - slot[p])
        fsend[it] = jnp.where(group % 2 == 0, fluxes[0], fluxes[1])
        fbuf[it, me] = fsend[it]

        @pl.loop(1, blocks)
        def _(d):
            remote(
                fsend.at[it], fbuf.at[it, me], phase_send.at[2 + it], phase_recv.at[2 + it],
                block_id(block_peer(d)),
            ).start()

    def spread_flux(it):
        whole(fbuf.at[it, pl.ds(0, blocks - 1)], 2 + it).wait_recv()
        seen = fbuf[it].reshape(blocks * 8, 128).astype(BF16)
        dense = jnp.zeros((lead, 128), F32)
        for p in range(2):
            half = select[p * blocks * 8 : (p + 1) * blocks * 8, :]
            every = lax.dot_general(seen, half, TN, preferred_element_type=F32)
            dense += every[lead * p : lead * p + lead, :]
        fall[it, row] = dense.astype(BF16)

        @pl.loop(1, n_row)
        def _(d):
            remote(
                fall.at[it, row], fall.at[it, row], phase_send.at[4 + it], phase_recv.at[4 + it],
                {"row": row_peer(d)},
            ).start()

    def new_share(it, old):
        whole(fall.at[it, pl.ds(0, n_row - 1)], 4 + it).wait_recv()
        if it == 0:
            whole(strip.at[pl.ds(0, n_row - 1)], 6).wait_recv()
        update = jnp.zeros((lead, share), F32)
        for r in range(n_row):
            update += jnp.dot(fall[it, r], strip[r], preferred_element_type=F32)
        return old + RELAXATION * update

    right_side(0)
    first_sweep(0, factors[0])
    halo_start(0)
    send_panel(5, 4)
    sweep(0, factors[1], False)
    halo_start(1)
    send_panel(9, 4)
    sweep(1, factors[2], False)
    halo_start(2)
    send_panel(13, n_row)
    sweep(2, factors[3], False, middle)
    send_flux(0, middle)
    halo_start(3)
    spread_flux(0)
    state = new_share(0, density[:, own])
    osend[0] = state
    rbuf[row] = state.astype(BF16)

    @pl.loop(1, n_row)
    def _(d):
        remote(
            rbuf.at[row], rbuf.at[row], phase_send.at[7], phase_recv.at[7], {"row": row_peer(d)}
        ).start()

    whole(rbuf.at[pl.ds(0, n_row - 1)], 7).wait_recv()

    send_potential(1, lambda k: rbuf[k])
    right_side(1)
    sweep(3, factors[0], False)
    halo_start(4)
    sweep(4, factors[1], False)
    halo_start(5)
    sweep(5, factors[2], False)
    halo_start(6)
    sweep(6, factors[3], True, inner)
    send_flux(1, inner)

    @pl.loop(0, 16, unroll=TURN)
    def _(i):
        x, y = i // 2, (i % 2) * 4
        tiles = quarters([inner[x, y + q] for q in range(4)])
        back = jnp.transpose(jnp.concatenate(tiles, axis=0))
        for q in range(4):
            volume_out[pl.ds(x * 8 + y + q, lead, stride=64), :] = back[lead * q : lead * q + lead, :]

    spread_flux(1)
    state = new_share(1, osend[0])
    osend[1] = state
    density_out[:, own] = state

    @pl.loop(1, n_row)
    def _(d):
        remote(
            osend.at[1], density_out.at[:, own], phase_send.at[8], phase_recv.at[8],
            {"row": row_peer(d)},
        ).start()

    whole(density_out.at[:, pl.ds(0, (n_row - 1) * share)], 8).wait_recv()

    for it in range(OUTER):
        whole(pbuf.at[it, pl.ds(0, blocks - 1)], it).wait_send()
        whole(fbuf.at[it, pl.ds(0, blocks - 1)], 2 + it).wait_send()
        whole(fall.at[it, pl.ds(0, n_row - 1)], 4 + it).wait_send()
    whole(strip.at[pl.ds(0, n_row - 1)], 6).wait_send()
    whole(rbuf.at[pl.ds(0, n_row - 1)], 7).wait_send()
    whole(density_out.at[:, pl.ds(0, (n_row - 1) * share)], 8).wait_send()
    for k in range(exchanges):
        halo_sent(k)


def local(panel, density, source, class_index, class_values, trace_count, trace_cell):
    sizes = (lax.axis_size("row"), lax.axis_size("col"), lax.axis_size("vol"))
    n_row, n_col, n_vol = sizes
    blocks = n_col * n_vol
    lead = source.shape[0]
    targets, nodes = panel.shape
    share = nodes // n_row
    ex = SWEEPS * OUTER - 1
    vmem = lambda shape, kind=F32: pltpu.VMEM(shape, kind)
    dma = pltpu.SemaphoreType.DMA
    density_out, volume = pl.pallas_call(
        functools.partial(kernel, sizes),
        out_shape=(
            jax.ShapeDtypeStruct(density.shape, F32),
            jax.ShapeDtypeStruct((lead * 64, 128), F32),
        ),
        in_specs=[pl.BlockSpec(memory_space=pltpu.VMEM)] * 4
        + [pl.BlockSpec(memory_space=pltpu.SMEM)] * 3,
        out_specs=(pl.BlockSpec(memory_space=pltpu.VMEM),) * 2,
        scratch_shapes=[
            vmem((blocks * SLOTS, targets), BF16),
            vmem((2048, 128), BF16),
            vmem((8, 8, 32, 128)),
            vmem((8, 8, 32, 128)),
            vmem((8, 8, 32, 128)),
            vmem((8, 8, 32, 128)),
            vmem((8, 8, 32, 128)),
            vmem((ex, 10, 10, 32, 128)),
            vmem((ex, 2, 2, 8, 128)),
            vmem((ex, 2, 8, 128)),
            vmem((ex, 2, 8, 128)),
            vmem((ex, 2, 8, 8, 128)),
            vmem((2, 8, 8, 128)),
            vmem((64, 128)),
            vmem((2, 8, 128)),
            vmem((SLOTS, 128)),
            vmem((OUTER, blocks, 8, 128)),
            vmem((OUTER, blocks, 8, 128)),
            vmem((OUTER, 8, 128)),
            vmem((OUTER, blocks, 8, 128)),
            vmem((OUTER, n_row, lead, targets), BF16),
            vmem((n_row, targets, share), BF16),
            vmem((n_row, lead, share), BF16),
            vmem((OUTER, lead, share)),
            dma((ex, 6)),
            dma((ex, 6)),
            dma((9,)),
            dma((9,)),
        ],
        compiler_params=pltpu.CompilerParams(
            collective_id=0, has_side_effects=True, vmem_limit_bytes=56 * 1024 * 1024
        ),
    )(
        panel,
        density,
        source.reshape(lead * 64, 128),
        class_index.reshape(64, 128),
        class_values,
        trace_count,
        trace_cell,
    )
    return density_out, volume.reshape(source.shape)


def solution(mesh):
    placed = (
        P("row", ("col", "vol")),
        P(None, ("col", "vol")),
        P(None, "row", "col", "vol"),
        P("row", "col", "vol"),
        P(),
        P("row", None),
        P("row", None, None),
    )
    return jax.shard_map(
        local,
        mesh=mesh,
        in_specs=placed,
        out_specs=(P(None, ("col", "vol")), P(None, "row", "col", "vol")),
        check_vma=False,
    )
```

time: 190 us -> 149 us (0.78)
  Pallas kernels: 183 us -> 143 us
    pallas_call x1, Pallas kernels: 183 us -> 143 us  [local(): pl.pallas_call(functools.partial(kernel, sizes), out_shape=(jax.ShapeDtyp...]
    unnamed x8 -> x5, local copies, waits for them, and re-layouts: 3.6 us -> 4.31 us
where the time goes in v1:
time: 149 us; the launch traced here: 148 us
  Pallas kernels  143 us (96%)
  local copies, waits for them, and re-layouts  4.31 us (3%)
    pallas_call x1, Pallas kernels, local(): pl.pallas_call(functools.partial(kernel, sizes), out_shape=(jax.ShapeDtyp...  143 us
    unnamed x5, local copies, waits for them, and re-layouts  4.31 us

profile of v1, /device:TPU:56, one launch (start us, length us, event | category | flops | bytes accessed | tf_op | source)
XLA Modules:
  0.0 148.3 jit_solution(3610708186225312932)
XLA Ops:
  0.6 1.4 copy.9.trace_cell
  2.0 143.3 %shard_map.86 = (f32[32,4096]{1,0:T(8,128)}, f32[2048,128]{1,0:T(8,128)}) custom-call(bf16[128,4096]{1,0:T(8,128)(2,1)} %panel.1, f32[32,4096]{1,0:T(8,128)} %density.1, f32[2048,128]{1,0:T(8,128)} %bitcast.3, s32[64,128]{1,0:T(8,128)} %bitcast.5, f32[16]{0:T(128)} %class_values.1, s32[1,32]{1,0:T(1,128)} %trace_count.1, s32[1,32,16]{2,1,0:T(8,128)} %copy.9.trace_cell), custom_call_target="tpu_custom_call" | custom-call | tf_op jit(solution)/shard_map/pallas_call | solution.py:505
  145.3 0.0 copy-start
  145.3 2.0 %copy.12 = f32[32,4096]{1,0:T(8,128)} copy(f32[32,4096]{1,0:T(8,128)} %get-tuple-element.8) | data formatting | bytes 1048576
  147.3 0.0 copy-done
  147.3 1.0 copy.13
Async XLA Ops:
  145.3 2.0 %copy-start = (f32[2048,128]{1,0:T(8,128)S(1)}, f32[2048,128]{1,0:T(8,128)}, u32[]{:S(2)}) copy-start(f32[2048,128]{1,0:T(8,128)} %get-tuple-element.5) | copy-start | bytes 3145732

commit v2 on v1

--- a/solution.py
+++ b/solution.py
@@ -39,7 +39,7 @@
     density_out, volume_out,
     select, hits, conduct, inverse, inner, middle, base, field, zface, zlo, zhi, zrow, zmix,
     turned, slot, picked, psend, pbuf, fsend, fbuf, fall, strip, rbuf, osend,
-    halo_send, halo_recv, phase_send, phase_recv,
+    halo_send, halo_recv, phase_send, phase_recv, gather_send, gather_recv,
 ):
     n_row, n_col, n_vol = sizes
     blocks = n_col * n_vol
@@ -183,15 +183,51 @@
             phase_send.at[6], phase_recv.at[6], {"row": r},
         )
 
-    def send_panel(first, count):
-        @pl.loop(first, min(first + count, n_row))
-        def _(d):
+    order = sorted(range(1, n_row), key=lambda d: -min(d, n_row - d))
+    head = max(1, n_row // 4)
+    rest = order[head:]
+    rest = [d for pair in zip(rest, reversed(rest)) for d in pair][: len(rest)]
+    batches = [order[:head]] + [rest[i::4] for i in range(4)]
+
+    def send_panel(i):
+        for d in batches[i]:
             panel_copy(d).start()
+
+    near = min(4, n_row)
+    far = n_row // near
+
+    def gather(i, cut):
+        def copy(r, peer):
+            return remote(
+                cut(r), cut(r), gather_send.at[i, r, peer], gather_recv.at[i, r], {"row": peer}
+            )
+
+        base_row = row - lax.rem(row, near)
+        nears = [base_row + lax.rem(row + d, near) for d in range(1, near)]
+        fars = [lax.rem(row + near * d, n_row) for d in range(1, far)]
+        for peer in fars + nears:
+            copy(row, peer).start()
+        for r in fars:
+            copy(r, row).wait_recv()
+            for peer in nears:
+                copy(r, peer).start()
+        for peer in nears:
+            for q in range(far):
+                copy(lax.rem(peer + near * q, n_row), row).wait_recv()
+
+        def sent():
+            for peer in fars + nears:
+                copy(row, peer).wait_send()
+            for r in fars:
+                for peer in nears:
+                    copy(r, peer).wait_send()
+
+        return sent
 
     own = pl.ds(pl.multiple_of(row * share, share), share)
     send_potential(0, lambda k: density[:, k * share : (k + 1) * share].astype(BF16))
     strip[row] = panel[:, own]
-    send_panel(1, 4)
+    send_panel(0)
 
     own_count = trace_count[0, me]
     cells, spot = [], jnp.full((8, 128), -1, jnp.int32)
@@ -425,28 +461,23 @@
     right_side(0)
     first_sweep(0, factors[0])
     halo_start(0)
-    send_panel(5, 4)
+    send_panel(1)
     sweep(0, factors[1], False)
     halo_start(1)
-    send_panel(9, 4)
+    send_panel(2)
     sweep(1, factors[2], False)
     halo_start(2)
-    send_panel(13, n_row)
+    send_panel(3)
     sweep(2, factors[3], False, middle)
     send_flux(0, middle)
     halo_start(3)
+    send_panel(4)
     spread_flux(0)
     state = new_share(0, density[:, own])
     osend[0] = state
     rbuf[row] = state.astype(BF16)
 
-    @pl.loop(1, n_row)
-    def _(d):
-        remote(
-            rbuf.at[row], rbuf.at[row], phase_send.at[7], phase_recv.at[7], {"row": row_peer(d)}
-        ).start()
-
-    whole(rbuf.at[pl.ds(0, n_row - 1)], 7).wait_recv()
+    sent_rounded = gather(0, lambda r: rbuf.at[r])
 
     send_potential(1, lambda k: rbuf[k])
     right_side(1)
@@ -469,25 +500,19 @@
 
     spread_flux(1)
     state = new_share(1, osend[0])
-    osend[1] = state
     density_out[:, own] = state
 
-    @pl.loop(1, n_row)
-    def _(d):
-        remote(
-            osend.at[1], density_out.at[:, own], phase_send.at[8], phase_recv.at[8],
-            {"row": row_peer(d)},
-        ).start()
-
-    whole(density_out.at[:, pl.ds(0, (n_row - 1) * share)], 8).wait_recv()
+    sent_final = gather(
+        1, lambda r: density_out.at[:, pl.ds(pl.multiple_of(r * share, share), share)]
+    )
 
     for it in range(OUTER):
         whole(pbuf.at[it, pl.ds(0, blocks - 1)], it).wait_send()
         whole(fbuf.at[it, pl.ds(0, blocks - 1)], 2 + it).wait_send()
         whole(fall.at[it, pl.ds(0, n_row - 1)], 4 + it).wait_send()
     whole(strip.at[pl.ds(0, n_row - 1)], 6).wait_send()
-    whole(rbuf.at[pl.ds(0, n_row - 1)], 7).wait_send()
-    whole(density_out.at[:, pl.ds(0, (n_row - 1) * share)], 8).wait_send()
+    sent_rounded()
+    sent_final()
     for k in range(exchanges):
         halo_sent(k)
 
@@ -535,11 +560,13 @@
             vmem((OUTER, n_row, lead, targets), BF16),
             vmem((n_row, targets, share), BF16),
             vmem((n_row, lead, share), BF16),
-            vmem((OUTER, lead, share)),
+            vmem((1, lead, share)),
             dma((ex, 6)),
             dma((ex, 6)),
-            dma((9,)),
-            dma((9,)),
+            dma((7,)),
+            dma((7,)),
+            dma((2, n_row, n_row)),
+            dma((2, n_row)),
         ],
         compiler_params=pltpu.CompilerParams(
             collective_id=0, has_side_effects=True, vmem_limit_bytes=56 * 1024 * 1024

time: 149 us -> 149 us (level)
  no operation moved by 1% of the time
where the time goes in v2:
time: 149 us; the launch traced here: 148 us
  Pallas kernels  143 us (96%)
  local copies, waits for them, and re-layouts  4.31 us (3%)
    pallas_call x1, Pallas kernels, local(): pl.pallas_call(functools.partial(kernel, sizes), out_shape=(jax.ShapeDtyp...  143 us
    unnamed x5, local copies, waits for them, and re-layouts  4.31 us

profile of v2, /device:TPU:56, one launch (start us, length us, event | category | flops | bytes accessed | tf_op | source)
XLA Modules:
  0.0 148.4 jit_solution(8839401013832161630)
XLA Ops:
  0.6 1.4 copy.9.trace_cell
  2.0 143.4 %shard_map.86 = (f32[32,4096]{1,0:T(8,128)}, f32[2048,128]{1,0:T(8,128)}) custom-call(bf16[128,4096]{1,0:T(8,128)(2,1)} %panel.1, f32[32,4096]{1,0:T(8,128)} %density.1, f32[2048,128]{1,0:T(8,128)} %bitcast.3, s32[64,128]{1,0:T(8,128)} %bitcast.5, f32[16]{0:T(128)} %class_values.1, s32[1,32]{1,0:T(1,128)} %trace_count.1, s32[1,32,16]{2,1,0:T(8,128)} %copy.9.trace_cell), custom_call_target="tpu_custom_call" | custom-call | tf_op jit(solution)/shard_map/pallas_call | solution.py:530
  145.4 0.0 copy-start
  145.4 2.0 %copy.12 = f32[32,4096]{1,0:T(8,128)} copy(f32[32,4096]{1,0:T(8,128)} %get-tuple-element.8) | data formatting | bytes 1048576
  147.4 0.0 copy-done
  147.4 1.0 copy.13
Async XLA Ops:
  145.4 2.0 %copy-start = (f32[2048,128]{1,0:T(8,128)S(1)}, f32[2048,128]{1,0:T(8,128)}, u32[]{:S(2)}) copy-start(f32[2048,128]{1,0:T(8,128)} %get-tuple-element.5) | copy-start | bytes 3145732

commit v3 on v2

--- a/solution.py
+++ b/solution.py
@@ -38,7 +38,7 @@
     panel, density, source, class_index, class_values, trace_count, trace_cell,
     density_out, volume_out,
     select, hits, conduct, inverse, inner, middle, base, field, zface, zlo, zhi, zrow, zmix,
-    turned, slot, picked, psend, pbuf, fsend, fbuf, fall, strip, rbuf, osend,
+    turned, slot, picked, psend, pbuf, fsend, fbuf, fall, strip, usend, urecv, rbuf, osend,
     halo_send, halo_recv, phase_send, phase_recv, gather_send, gather_recv,
 ):
     n_row, n_col, n_vol = sizes
@@ -176,25 +176,29 @@
                 psend.at[it, j], pbuf.at[it, me], phase_send.at[it], phase_recv.at[it], block_id(j)
             ).start()
 
-    def panel_copy(d):
-        r = row_peer(d)
+    near = min(4, n_row)
+    far = n_row // near
+
+    base_row = row - lax.rem(row, near)
+    mine_near = lax.rem(row, near)
+    mine_far = row // near
+    nears = [base_row + lax.rem(row + d, near) for d in range(1, near)]
+    fars = [lax.rem(row + near * d, n_row) for d in range(1, far)]
+
+    def panel_copy(d, f):
+        r = base_row + lax.rem(row + d, near)
+        at = (near * f + lax.rem(r, near)) * share
         return remote(
-            panel.at[:, pl.ds(pl.multiple_of(r * share, share), share)], strip.at[row],
+            panel.at[:, pl.ds(pl.multiple_of(at, share), share)], strip.at[mine_near, f],
             phase_send.at[6], phase_recv.at[6], {"row": r},
         )
 
-    order = sorted(range(1, n_row), key=lambda d: -min(d, n_row - d))
-    head = max(1, n_row // 4)
-    rest = order[head:]
-    rest = [d for pair in zip(rest, reversed(rest)) for d in pair][: len(rest)]
-    batches = [order[:head]] + [rest[i::4] for i in range(4)]
+    chunks = [(d, f) for f in range(far) for d in range(1, near)]
+    per = (len(chunks) + 3) // 4
 
     def send_panel(i):
-        for d in batches[i]:
-            panel_copy(d).start()
-
-    near = min(4, n_row)
-    far = n_row // near
+        for d, f in chunks[i * per : (i + 1) * per]:
+            panel_copy(d, f).start()
 
     def gather(i, cut):
         def copy(r, peer):
@@ -202,9 +206,6 @@
                 cut(r), cut(r), gather_send.at[i, r, peer], gather_recv.at[i, r], {"row": peer}
             )
 
-        base_row = row - lax.rem(row, near)
-        nears = [base_row + lax.rem(row + d, near) for d in range(1, near)]
-        fars = [lax.rem(row + near * d, n_row) for d in range(1, far)]
         for peer in fars + nears:
             copy(row, peer).start()
         for r in fars:
@@ -226,7 +227,9 @@
 
     own = pl.ds(pl.multiple_of(row * share, share), share)
     send_potential(0, lambda k: density[:, k * share : (k + 1) * share].astype(BF16))
-    strip[row] = panel[:, own]
+    for f in range(far):
+        at = (near * f + mine_near) * share
+        strip[mine_near, f] = panel[:, pl.ds(pl.multiple_of(at, share), share)]
     send_panel(0)
 
     own_count = trace_count[0, me]
@@ -440,22 +443,34 @@
             half = select[p * blocks * 8 : (p + 1) * blocks * 8, :]
             every = lax.dot_general(seen, half, TN, preferred_element_type=F32)
             dense += every[lead * p : lead * p + lead, :]
-        fall[it, row] = dense.astype(BF16)
-
-        @pl.loop(1, n_row)
-        def _(d):
+        fall[it, mine_near] = dense.astype(BF16)
+        for peer in nears:
             remote(
-                fall.at[it, row], fall.at[it, row], phase_send.at[4 + it], phase_recv.at[4 + it],
-                {"row": row_peer(d)},
+                fall.at[it, mine_near], fall.at[it, mine_near], phase_send.at[4 + it],
+                phase_recv.at[4 + it], {"row": peer},
             ).start()
 
     def new_share(it, old):
-        whole(fall.at[it, pl.ds(0, n_row - 1)], 4 + it).wait_recv()
+        whole(fall.at[it, pl.ds(0, near - 1)], 4 + it).wait_recv()
         if it == 0:
-            whole(strip.at[pl.ds(0, n_row - 1)], 6).wait_recv()
-        update = jnp.zeros((lead, share), F32)
-        for r in range(n_row):
-            update += jnp.dot(fall[it, r], strip[r], preferred_element_type=F32)
+            whole(strip.at[pl.ds(0, near - 1)], 6).wait_recv()
+        for f in range(far):
+            update = jnp.zeros((lead, share), F32)
+            for n in range(near):
+                update += jnp.dot(fall[it, n], strip[n, f], preferred_element_type=F32)
+            usend[it, f] = update
+        urecv[it, mine_far] = usend[it, mine_far]
+        for d in range(1, far):
+            f = lax.rem(mine_far + d, far)
+            remote(
+                usend.at[it, f], urecv.at[it, mine_far], phase_send.at[7 + it],
+                phase_recv.at[7 + it], {"row": lax.rem(row + near * d, n_row)},
+            ).start()
+        if far > 1:
+            whole(urecv.at[it, pl.ds(0, far - 1)], 7 + it).wait_recv()
+        update = urecv[it, 0]
+        for f in range(1, far):
+            update += urecv[it, f]
         return old + RELAXATION * update
 
     right_side(0)
@@ -471,7 +486,6 @@
     sweep(2, factors[3], False, middle)
     send_flux(0, middle)
     halo_start(3)
-    send_panel(4)
     spread_flux(0)
     state = new_share(0, density[:, own])
     osend[0] = state
@@ -509,8 +523,10 @@
     for it in range(OUTER):
         whole(pbuf.at[it, pl.ds(0, blocks - 1)], it).wait_send()
         whole(fbuf.at[it, pl.ds(0, blocks - 1)], 2 + it).wait_send()
-        whole(fall.at[it, pl.ds(0, n_row - 1)], 4 + it).wait_send()
-    whole(strip.at[pl.ds(0, n_row - 1)], 6).wait_send()
+        whole(fall.at[it, pl.ds(0, near - 1)], 4 + it).wait_send()
+        if far > 1:
+            whole(urecv.at[it, pl.ds(0, far - 1)], 7 + it).wait_send()
+    whole(strip.at[pl.ds(0, near - 1)], 6).wait_send()
     sent_rounded()
     sent_final()
     for k in range(exchanges):
@@ -524,6 +540,7 @@
     lead = source.shape[0]
     targets, nodes = panel.shape
     share = nodes // n_row
+    near = min(4, n_row)
     ex = SWEEPS * OUTER - 1
     vmem = lambda shape, kind=F32: pltpu.VMEM(shape, kind)
     dma = pltpu.SemaphoreType.DMA
@@ -557,14 +574,16 @@
             vmem((OUTER, blocks, 8, 128)),
             vmem((OUTER, 8, 128)),
             vmem((OUTER, blocks, 8, 128)),
-            vmem((OUTER, n_row, lead, targets), BF16),
-            vmem((n_row, targets, share), BF16),
+            vmem((OUTER, near, lead, targets), BF16),
+            vmem((near, n_row // near, targets, share), BF16),
+            vmem((OUTER, n_row // near, lead, share)),
+            vmem((OUTER, n_row // near, lead, share)),
             vmem((n_row, lead, share), BF16),
             vmem((1, lead, share)),
             dma((ex, 6)),
             dma((ex, 6)),
-            dma((7,)),
-            dma((7,)),
+            dma((9,)),
+            dma((9,)),
             dma((2, n_row, n_row)),
             dma((2, n_row)),
         ],

time: 149 us -> 138 us (0.926)
  Pallas kernels: 143 us -> 132 us
    pallas_call x1, Pallas kernels: 143 us -> 132 us  [local(): pl.pallas_call(functools.partial(kernel, sizes), out_shape=(jax.ShapeDtyp...]
where the time goes in v3:
time: 138 us; the launch traced here: 137 us
  Pallas kernels  132 us (96%)
  local copies, waits for them, and re-layouts  4.31 us (3%)
    pallas_call x1, Pallas kernels, local(): pl.pallas_call(functools.partial(kernel, sizes), out_shape=(jax.ShapeDtyp...  132 us
    unnamed x5, local copies, waits for them, and re-layouts  4.31 us

profile of v3, /device:TPU:56, one launch (start us, length us, event | category | flops | bytes accessed | tf_op | source)
XLA Modules:
  0.0 137.4 jit_solution(15685770249767850964)
XLA Ops:
  0.6 1.4 %copy.9.trace_cell = s32[1,32,16]{2,1,0:T(8,128)} copy(s32[1,32,16]{1,2,0:T(8,128)} %param.13) | data formatting | bytes 4096 | tf_op args[6]
  2.0 132.5 %shard_map.86 = (f32[32,4096]{1,0:T(8,128)}, f32[2048,128]{1,0:T(8,128)}) custom-call(bf16[128,4096]{1,0:T(8,128)(2,1)} %panel.1, f32[32,4096]{1,0:T(8,128)} %density.1, f32[2048,128]{1,0:T(8,128)} %bitcast.3, s32[64,128]{1,0:T(8,128)} %bitcast.5, f32[16]{0:T(128)} %class_values.1, s32[1,32]{1,0:T(1,128)} %trace_count.1, s32[1,32,16]{2,1,0:T(8,128)} %copy.9.trace_cell), custom_call_target="tpu_custom_call" | custom-call | tf_op jit(solution)/shard_map/pallas_call | solution.py:547
  134.5 0.0 copy-start
  134.5 2.0 %copy.12 = f32[32,4096]{1,0:T(8,128)} copy(f32[32,4096]{1,0:T(8,128)} %get-tuple-element.8) | data formatting | bytes 1048576
  136.5 0.0 copy-done
  136.5 1.0 copy.13
Async XLA Ops:
  134.5 2.0 %copy-start = (f32[2048,128]{1,0:T(8,128)S(1)}, f32[2048,128]{1,0:T(8,128)}, u32[]{:S(2)}) copy-start(f32[2048,128]{1,0:T(8,128)} %get-tuple-element.5) | copy-start | bytes 3145732

commit v4 on v3

--- a/solution.py
+++ b/solution.py
@@ -54,17 +54,23 @@
     def block_id(j):
         return {"col": j // n_vol, "vol": j % n_vol}
 
-    def block_peer(d):
-        return lax.rem(me + d, blocks)
+    def steps(size):
+        return sorted(range(size), key=lambda d: (-min(d, size - d), d))
+
+    block_steps = [(c, v) for v in steps(n_vol) for c in steps(n_col) if (c, v) != (0, 0)]
+
+    def block_peer(step):
+        return lax.rem(col + step[0], n_col) * n_vol + lax.rem(vol + step[1], n_vol)
 
     def row_peer(d):
         return lax.rem(row + d, n_row)
 
     barrier = pltpu.get_barrier_semaphore()
 
-    @pl.loop(1, blocks)
-    def _(d):
-        pl.semaphore_signal(barrier, inc=1, device_id=block_id(block_peer(d)), device_id_type=MESH)
+    for step in block_steps:
+        pl.semaphore_signal(
+            barrier, inc=1, device_id=block_id(block_peer(step)), device_id_type=MESH
+        )
 
     @pl.loop(1, n_row)
     def _(d):
@@ -169,9 +175,8 @@
             pl.semaphore_wait(barrier, blocks - 1 + n_row - 1)
         pbuf[it, me] = psend[it, me]
 
-        @pl.loop(1, blocks)
-        def _(d):
-            j = block_peer(d)
+        for step in block_steps:
+            j = block_peer(step)
             remote(
                 psend.at[it, j], pbuf.at[it, me], phase_send.at[it], phase_recv.at[it], block_id(j)
             ).start()
@@ -194,10 +199,10 @@
         )
 
     chunks = [(d, f) for f in range(far) for d in range(1, near)]
-    per = (len(chunks) + 3) // 4
+    cuts = [len(chunks) * part // 12 for part in (0, 6, 8, 10, 12)]
 
     def send_panel(i):
-        for d, f in chunks[i * per : (i + 1) * per]:
+        for d, f in chunks[cuts[i] : cuts[i + 1]]:
             panel_copy(d, f).start()
 
     def gather(i, cut):
@@ -323,16 +328,28 @@
                     packed = jnp.where(group == i, moved, packed)
                 zface[k, side, b] = packed
 
+    def ends_first(plane, between):
+        @pl.loop(0, 2)
+        def _(i):
+            plane(7 * i)
+
+        between()
+
+        @pl.loop(1, 7)
+        def _(x):
+            plane(x)
+
     def first_sweep(k, factor):
-        @pl.loop(0, 8)
-        def _(x):
+        def plane(x):
             packed = (jnp.zeros((8, 128), F32),) * 2
             for y in range(8):
                 new = [factor * base[x, y, SPANS[b], :] for b in range(4)]
                 packed = keep(k, x, y, new, packed)
             zrow[k, 0, x], zrow[k, 1, x] = packed
 
+        ends_first(plane, lambda: halo_start(k, (0, 1)))
         pack_rows(k)
+        halo_start(k, (4, 5, 2, 3))
 
     def halo_copies(k):
         pairs = (
@@ -350,9 +367,9 @@
 
     arrives = (row > 0, row < n_row - 1, col > 0, col < n_col - 1, vol > 0, vol < n_vol - 1)
 
-    def halo_start(k):
+    def halo_start(k, which):
         copies = halo_copies(k)
-        for i in (4, 5, 0, 1, 2, 3):
+        for i in which:
             @pl.when(copies[i][0])
             def _(copy=copies[i][1]):
                 copy.start()
@@ -379,8 +396,7 @@
             zmix[0, x] = pltpu.roll(jnp.where(group == 3, low, zrow[k, 1, x]), 32, 1)
             zmix[1, x] = pltpu.roll(jnp.where(group == 0, top, zrow[k, 0, x]), 96, 1)
 
-        @pl.loop(0, 8)
-        def _(x):
+        def plane(x):
             packed = (jnp.zeros((8, 128), F32),) * 2
             for y in range(8):
                 c = [field[k, x + 1, y + 1, SPANS[b], :] for b in range(4)]
@@ -410,8 +426,13 @@
             if not last:
                 zrow[k + 1, 0, x], zrow[k + 1, 1, x] = packed
 
-        if not last:
+        if last:
+            pl.loop(0, 8)(plane)
+        else:
+            ends_first(plane, lambda: halo_start(k + 1, (0, 1)))
             pack_rows(k + 1)
+            if seen is None:
+                halo_start(k + 1, (4, 5, 2, 3))
 
     def send_flux(it, ref):
         for s in range(SLOTS):
@@ -428,11 +449,10 @@
         fsend[it] = jnp.where(group % 2 == 0, fluxes[0], fluxes[1])
         fbuf[it, me] = fsend[it]
 
-        @pl.loop(1, blocks)
-        def _(d):
+        for step in block_steps:
             remote(
                 fsend.at[it], fbuf.at[it, me], phase_send.at[2 + it], phase_recv.at[2 + it],
-                block_id(block_peer(d)),
+                block_id(block_peer(step)),
             ).start()
 
     def spread_flux(it):
@@ -475,17 +495,14 @@
 
     right_side(0)
     first_sweep(0, factors[0])
-    halo_start(0)
     send_panel(1)
     sweep(0, factors[1], False)
-    halo_start(1)
     send_panel(2)
     sweep(1, factors[2], False)
-    halo_start(2)
     send_panel(3)
     sweep(2, factors[3], False, middle)
     send_flux(0, middle)
-    halo_start(3)
+    halo_start(3, (4, 5, 2, 3))
     spread_flux(0)
     state = new_share(0, density[:, own])
     osend[0] = state
@@ -496,11 +513,8 @@
     send_potential(1, lambda k: rbuf[k])
     right_side(1)
     sweep(3, factors[0], False)
-    halo_start(4)
     sweep(4, factors[1], False)
-    halo_start(5)
     sweep(5, factors[2], False)
-    halo_start(6)
     sweep(6, factors[3], True, inner)
     send_flux(1, inner)
 

time: 138 us -> 140 us (1.014)
  Pallas kernels: 132 us -> 134 us
    pallas_call x1, Pallas kernels: 132 us -> 134 us  [local(): pl.pallas_call(functools.partial(kernel, sizes), out_shape=(jax.ShapeDtyp...]
where the time goes in v4:
time: 140 us; the launch traced here: 139 us
  Pallas kernels  134 us (96%)
  local copies, waits for them, and re-layouts  4.31 us (3%)
    pallas_call x1, Pallas kernels, local(): pl.pallas_call(functools.partial(kernel, sizes), out_shape=(jax.ShapeDtyp...  134 us
    unnamed x5, local copies, waits for them, and re-layouts  4.31 us

profile of v4, /device:TPU:56, one launch (start us, length us, event | category | flops | bytes accessed | tf_op | source)
XLA Modules:
  0.0 139.0 jit_solution(11376525628759986187)
XLA Ops:
  0.6 1.4 copy.9.trace_cell
  2.0 134.0 %shard_map.86 = (f32[32,4096]{1,0:T(8,128)}, f32[2048,128]{1,0:T(8,128)}) custom-call(bf16[128,4096]{1,0:T(8,128)(2,1)} %panel.1, f32[32,4096]{1,0:T(8,128)} %density.1, f32[2048,128]{1,0:T(8,128)} %bitcast.3, s32[64,128]{1,0:T(8,128)} %bitcast.5, f32[16]{0:T(128)} %class_values.1, s32[1,32]{1,0:T(1,128)} %trace_count.1, s32[1,32,16]{2,1,0:T(8,128)} %copy.9.trace_cell), custom_call_target="tpu_custom_call" | custom-call | tf_op jit(solution)/shard_map/pallas_call | solution.py:561
  136.0 0.0 copy-start
  136.0 2.0 %copy.12 = f32[32,4096]{1,0:T(8,128)} copy(f32[32,4096]{1,0:T(8,128)} %get-tuple-element.8) | data formatting | bytes 1048576
  138.0 0.0 copy-done
  138.0 1.0 copy.13
Async XLA Ops:
  136.0 2.0 %copy-start = (f32[2048,128]{1,0:T(8,128)S(1)}, f32[2048,128]{1,0:T(8,128)}, u32[]{:S(2)}) copy-start(f32[2048,128]{1,0:T(8,128)} %get-tuple-element.5) | copy-start | bytes 3145732

commit v5 on v4

--- a/solution.py
+++ b/solution.py
@@ -54,23 +54,17 @@
     def block_id(j):
         return {"col": j // n_vol, "vol": j % n_vol}
 
-    def steps(size):
-        return sorted(range(size), key=lambda d: (-min(d, size - d), d))
-
-    block_steps = [(c, v) for v in steps(n_vol) for c in steps(n_col) if (c, v) != (0, 0)]
-
-    def block_peer(step):
-        return lax.rem(col + step[0], n_col) * n_vol + lax.rem(vol + step[1], n_vol)
+    def block_peer(d):
+        return lax.rem(me + d, blocks)
 
     def row_peer(d):
         return lax.rem(row + d, n_row)
 
     barrier = pltpu.get_barrier_semaphore()
 
-    for step in block_steps:
-        pl.semaphore_signal(
-            barrier, inc=1, device_id=block_id(block_peer(step)), device_id_type=MESH
-        )
+    @pl.loop(1, blocks)
+    def _(d):
+        pl.semaphore_signal(barrier, inc=1, device_id=block_id(block_peer(d)), device_id_type=MESH)
 
     @pl.loop(1, n_row)
     def _(d):
@@ -175,8 +169,9 @@
             pl.semaphore_wait(barrier, blocks - 1 + n_row - 1)
         pbuf[it, me] = psend[it, me]
 
-        for step in block_steps:
-            j = block_peer(step)
+        @pl.loop(1, blocks)
+        def _(d):
+            j = block_peer(d)
             remote(
                 psend.at[it, j], pbuf.at[it, me], phase_send.at[it], phase_recv.at[it], block_id(j)
             ).start()
@@ -199,10 +194,10 @@
         )
 
     chunks = [(d, f) for f in range(far) for d in range(1, near)]
-    cuts = [len(chunks) * part // 12 for part in (0, 6, 8, 10, 12)]
+    per = (len(chunks) + 3) // 4
 
     def send_panel(i):
-        for d, f in chunks[cuts[i] : cuts[i + 1]]:
+        for d, f in chunks[i * per : (i + 1) * per]:
             panel_copy(d, f).start()
 
     def gather(i, cut):
@@ -449,10 +444,11 @@
         fsend[it] = jnp.where(group % 2 == 0, fluxes[0], fluxes[1])
         fbuf[it, me] = fsend[it]
 
-        for step in block_steps:
+        @pl.loop(1, blocks)
+        def _(d):
             remote(
                 fsend.at[it], fbuf.at[it, me], phase_send.at[2 + it], phase_recv.at[2 + it],
-                block_id(block_peer(step)),
+                block_id(block_peer(d)),
             ).start()
 
     def spread_flux(it):

time: 140 us -> 141 us (level)
  no operation moved by 1% of the time
where the time goes in v5:
time: 141 us; the launch traced here: 140 us
  Pallas kernels  135 us (96%)
  local copies, waits for them, and re-layouts  4.31 us (3%)
    pallas_call x1, Pallas kernels, local(): pl.pallas_call(functools.partial(kernel, sizes), out_shape=(jax.ShapeDtyp...  135 us
    unnamed x5, local copies, waits for them, and re-layouts  4.31 us

profile of v5, /device:TPU:56, one launch (start us, length us, event | category | flops | bytes accessed | tf_op | source)
XLA Modules:
  0.0 139.7 jit_solution(3113720234316342539)
XLA Ops:
  0.6 1.4 copy.9.trace_cell
  2.0 134.8 %shard_map.86 = (f32[32,4096]{1,0:T(8,128)}, f32[2048,128]{1,0:T(8,128)}) custom-call(bf16[128,4096]{1,0:T(8,128)(2,1)} %panel.1, f32[32,4096]{1,0:T(8,128)} %density.1, f32[2048,128]{1,0:T(8,128)} %bitcast.3, s32[64,128]{1,0:T(8,128)} %bitcast.5, f32[16]{0:T(128)} %class_values.1, s32[1,32]{1,0:T(1,128)} %trace_count.1, s32[1,32,16]{2,1,0:T(8,128)} %copy.9.trace_cell), custom_call_target="tpu_custom_call" | custom-call | tf_op jit(solution)/shard_map/pallas_call | solution.py:557
  136.8 0.0 copy-start
  136.8 2.0 %copy.12 = f32[32,4096]{1,0:T(8,128)} copy(f32[32,4096]{1,0:T(8,128)} %get-tuple-element.8) | data formatting | bytes 1048576
  138.7 0.0 copy-done
  138.7 1.0 copy.13
Async XLA Ops:
  136.8 2.0 %copy-start = (f32[2048,128]{1,0:T(8,128)S(1)}, f32[2048,128]{1,0:T(8,128)}, u32[]{:S(2)}) copy-start(f32[2048,128]{1,0:T(8,128)} %get-tuple-element.5) | copy-start | bytes 3145732
